TPU v7x, 32 devices: a whole 2x2x4 slice. The times are simulated.
32 devices in a mesh: dp: 4 (over y, x), fsdp: 8 (over z, core).
Axes of the slice: x: 2, y: 2, z: 4, core: 2. Of those that a mesh axis runs over, the one named last changes fastest.
Arguments:
- input_tokens: int32 [2, 32768], P(None, ('dp', 'fsdp')), may hold values from 0 to 29
- item_numbers: int32 [2, 32768], P(None, ('dp', 'fsdp')), may hold values from -1 to 3, as said below
- loss_positions: int32 [2, 4096], P(None, ('dp', 'fsdp')), may hold values from -1 to 1023, as said below
- target_tokens: int32 [2, 4096], P(None, ('dp', 'fsdp')), may hold values from 0 to 29
- input_projection: float32 [1280, 640], P('fsdp', 'dp'), may hold values from -0.15625 to 0.15625
- dilated_conv: float32 [3200, 640], P('fsdp', 'dp'), may hold values from -0.109375 to 0.109375
- output_projection: float32 [1280, 640], P('fsdp', 'dp'), may hold values from -0.25 to 0.25
- vectors: float32 [68, 1280], P(None, ('dp', 'fsdp'))
- input_first_moment: float32 [1280, 640], P('fsdp'), may hold values from -6.67572e-06 to 6.67572e-06
- input_second_moment: float32 [1280, 640], P('fsdp'), may hold values from 5.3002034e-12 to 2.1200814e-11
- conv_first_moment: float32 [3200, 640], P('fsdp'), may hold values from -6.67572e-06 to 6.67572e-06
- conv_second_moment: float32 [3200, 640], P('fsdp'), may hold values from 5.3002034e-12 to 2.1200814e-11
- output_first_moment: float32 [1280, 640], P('fsdp'), may hold values from -6.67572e-06 to 6.67572e-06
- output_second_moment: float32 [1280, 640], P('fsdp'), may hold values from 5.3002034e-12 to 2.1200814e-11
- vector_first_moment: float32 [68, 1280], P(None, ('dp', 'fsdp')), may hold values from -1.9073486e-05 to 1.9073486e-05
- vector_second_moment: float32 [68, 1280], P(None, ('dp', 'fsdp')), may hold values from 4.7701832e-11 to 1.9080733e-10
- bases: float32 [3, 640, 640], replicated, as said below
- eigenbasis_flags: int32 [3], replicated, may hold values from 0 to 1, as said below
- optimizer_step: int32 [1], replicated, may hold values from 2 to 20
Outputs:
- mean_loss: float32 [], replicated
- grad_norm: float32 [], replicated
- master_in: float32 [1280, 640], P('fsdp', 'dp')
- copy_in: bfloat16 [1280, 640], P('fsdp', 'dp')
- moment_in: float32 [1280, 640], P('fsdp')
- square_in: float32 [1280, 640], P('fsdp')
- updated_conv: float32 [3200, 640], P('fsdp', 'dp')
- conv_bfloat_copy: bfloat16 [3200, 640], P('fsdp', 'dp')
- updated_conv_moment: float32 [3200, 640], P('fsdp')
- updated_conv_square: float32 [3200, 640], P('fsdp')
- master_out: float32 [1280, 640], P('fsdp', 'dp')
- copy_out: bfloat16 [1280, 640], P('fsdp', 'dp')
- moment_out: float32 [1280, 640], P('fsdp')
- square_out: float32 [1280, 640], P('fsdp')
- master_vec: float32 [68, 1280], P(None, ('dp', 'fsdp'))
- copy_vec: bfloat16 [68, 1280], P(None, ('dp', 'fsdp'))
- moment_vec: float32 [68, 1280], P(None, ('dp', 'fsdp'))
- square_vec: float32 [68, 1280], P(None, ('dp', 'fsdp'))
Inputs may be any that keep to these rules, and one draw needn't show every extreme that they name: `item_numbers`: each device's 1024 slots of a micro-batch hold whole items of 256, 512 or 1024 tokens, numbered from 0 in order and starting at slot 0, followed by padding marked -1; items fill at least half of the slots; some device holds one item of 1024 tokens. `loss_positions`: slot i of a device's 128 slots in a micro-batch holds -1 or a position from 8 i to 8 i + 7 of that device's slots; it holds a position exactly when that position belongs to an item. `eigenbasis_flags`: two of the three entries are 1. `bases`: each matrix is orthogonal.
All inputs are finite; a program needn't handle non-finite values.
Results may differ from a plain program's by a relative error of at most 0.0091.
Values may be sent and summed in bfloat16 or wider, within the bound.
A program may use at most 256 MiB of HBM per device.

v0:
```python
from functools import partial

import jax
import jax.numpy as jnp
from jax import lax
from jax.experimental import pallas as pl
from jax.experimental.pallas import tpu as pltpu
from jax.sharding import PartitionSpec as P

VOCAB = 30
CONV_TAPS = 5
DILATION = 8
TABLE = 32
MESH = pl.DeviceIdType.MESH


beta_one = 0.9
beta_two = 0.95
epsilon = 1e-08
rate_matrix = 0.02
rate_vector = 0.5
decay_weight = 0.01
clip_limit = 0.02
norm_eps = 1e-05
highest_precision = lax.Precision.HIGHEST


def layer_norm(values, norm_gain, norm_bias):
    centre = values - jnp.mean(values, axis=-1, keepdims=True)
    spread = jnp.mean(centre * centre, axis=-1, keepdims=True)
    return centre * lax.rsqrt(spread + norm_eps) * norm_gain + norm_bias


def norm_gelu(values, norm_gain, norm_bias):
    return jax.nn.gelu(layer_norm(values, norm_gain, norm_bias), approximate=True)


def moved_groups(values, step):
    if step > 0:
        return jnp.concatenate([values[:, step:], jnp.full_like(values[:, :step], -1)], axis=1)
    if step < 0:
        return jnp.concatenate([jnp.full_like(values[:, :-step], -1), values[:, :step]], axis=1)
    return values


def tap_onehots(tokens, items, positions):
    batches, slots = positions.shape
    stride = tokens.shape[1] // slots
    token_groups = tokens.reshape(batches, slots, stride)
    item_groups = items.reshape(batches, slots, stride)
    valid = positions >= 0
    residue = jnp.where(valid, positions - stride * jnp.arange(slots, dtype=jnp.int32)[None], -1)
    chosen = residue[:, :, None] == jnp.arange(stride, dtype=jnp.int32)[None, None]
    own_item = jnp.sum(jnp.where(chosen, item_groups, 0), axis=2)
    identities = jnp.arange(TABLE, dtype=jnp.int32)
    result = []
    for tap in range(CONV_TAPS):
        step = (tap - CONV_TAPS // 2) * DILATION // stride
        item = jnp.sum(jnp.where(chosen, moved_groups(item_groups, step), 0), axis=2)
        token = jnp.sum(jnp.where(chosen, moved_groups(token_groups, step), 0), axis=2)
        keep = valid & (item == own_item) & (own_item >= 0)
        result.append(jnp.where(keep, token, -1)[:, :, None] == identities)
    return jnp.concatenate(result, axis=2).reshape(batches * slots, CONV_TAPS * TABLE)


def exact_dot(left, right, contract):
    high = left.astype(jnp.bfloat16)
    low = (left - high.astype(jnp.float32)).astype(jnp.bfloat16)
    return lax.dot_general(high, right, contract, preferred_element_type=jnp.float32) + lax.dot_general(
        low, right, contract, preferred_element_type=jnp.float32
    )


def column_sum(values):
    return jnp.sum(values, axis=0, dtype=jnp.float32)


def split_two(count):
    high = int(count**0.5)
    while count % high:
        high -= 1
    return high, count // high


def spread_peers(dp_size, fsdp_size):
    high, low = split_two(dp_size)
    depth = fsdp_size // 2
    me_dp, me_fsdp = lax.axis_index("dp"), lax.axis_index("fsdp")
    z, core = me_fsdp // 2, lax.rem(me_fsdp, 2)
    y, x = me_dp // low, lax.rem(me_dp, low)
    along_z = [lax.rem(z + i, depth) for i in range(1, depth)]
    along_y = [lax.rem(y + i, high) for i in range(1, high)]
    along_x = [lax.rem(x + i, low) for i in range(1, low)]
    return (z, y, x, core, low, along_z, along_y, along_x)


def meet(peers):
    barrier = pltpu.get_barrier_semaphore()
    for peer in peers:
        pl.semaphore_signal(barrier, inc=1, device_id=peer, device_id_type=MESH)
    pl.semaphore_wait(barrier, len(peers))


def gather_kernel(
    dp_size, fsdp_size, cut, shard_ref, vec_ref, out_ref, vec_out_ref, send_sem, recv_sem, own_sem
):
    z, y, x, core, low, along_z, along_y, along_x = spread_peers(dp_size, fsdp_size)
    me_dp, me_fsdp = y * low + x, z * 2 + core
    z_ids = [(me_dp, other * 2 + core) for other in along_z]
    y_ids = [(other * low + x, me_fsdp) for other in along_y]
    x_ids = [(y * low + other, me_fsdp) for other in along_x]
    partner = (me_dp, z * 2 + 1 - core)
    meet(z_ids + y_ids + x_ids + [partner])
    parts = ((0, cut), (cut, shard_ref.shape[0] - cut))

    def place(piece, column, row):
        if piece == 0:
            return vec_out_ref.at[column, row]
        begin, size = parts[piece - 1]
        return out_ref.at[row, column, pl.ds(begin, size)]

    def source(piece):
        if piece == 0:
            return vec_ref
        begin, size = parts[piece - 1]
        return shard_ref.at[pl.ds(begin, size)]

    started = []

    def push(piece, column, row, held, peers):
        for peer in peers:
            copy = pltpu.make_async_remote_copy(
                src_ref=held,
                dst_ref=place(piece, column, row),
                send_sem=send_sem.at[len(started)],
                recv_sem=recv_sem.at[piece, column, row],
                device_id=peer,
                device_id_type=MESH,
            )
            copy.start()
            started.append(copy)

    def arrived(piece, column, row):
        block = place(piece, column, row)
        pltpu.make_async_remote_copy(
            src_ref=block,
            dst_ref=block,
            send_sem=send_sem.at[0],
            recv_sem=recv_sem.at[piece, column, row],
            device_id=partner,
            device_id_type=MESH,
        ).wait_recv()
        return block

    def dims(piece):
        if piece == 2:
            return (along_y, y_ids, True), (along_x, x_ids, False)
        return (along_x, x_ids, False), (along_y, y_ids, True)

    kept = []
    for piece in range(3):
        copy = pltpu.make_async_copy(source(piece), place(piece, me_dp, me_fsdp), own_sem.at[piece])
        copy.start()
        kept.append(copy)
        first, second = dims(piece)
        push(piece, me_dp, me_fsdp, source(piece), z_ids + first[1] + second[1] + [partner])
    for other in along_z:
        for piece in range(3):
            first, second = dims(piece)
            row = other * 2 + core
            push(piece, me_dp, row, arrived(piece, me_dp, row), first[1] + second[1] + [partner])
    all_z = [z] + along_z
    for other in all_z:
        for piece in range(3):
            first, second = dims(piece)
            row = other * 2 + core
            for place_one in first[0]:
                column = place_one * low + x if first[2] else y * low + place_one
                push(piece, column, row, arrived(piece, column, row), second[1] + [partner])
    for other in all_z:
        for piece in range(3):
            first, second = dims(piece)
            own_first = y if first[2] else x
            row = other * 2 + core
            for place_two in second[0]:
                for place_one in [own_first] + first[0]:
                    column = (
                        place_one * low + place_two if first[2] else place_two * low + place_one
                    )
                    push(piece, column, row, arrived(piece, column, row), [partner])
    for other in all_z:
        for piece in range(3):
            for place_y in [y] + along_y:
                for place_x in [x] + along_x:
                    arrived(piece, place_y * low + place_x, other * 2 + 1 - core)
    for copy in kept:
        copy.wait()
    for copy in started:
        copy.wait_send()


def gather_all(shard, vec_shard, dp_size, fsdp_size):
    cut = shard.shape[0] // 2 // 16 * 16
    high, low = split_two(dp_size)
    depth = fsdp_size // 2
    sends = 0
    for first, second in ((low, high), (low, high), (high, low)):
        sends += (depth - 1) + depth * (first - 1) + depth * first * (second - 1)
        sends += depth * first * second
    return pl.pallas_call(
        partial(gather_kernel, dp_size, fsdp_size, cut),
        out_shape=(
            jax.ShapeDtypeStruct((fsdp_size, dp_size) + shard.shape, shard.dtype),
            jax.ShapeDtypeStruct((dp_size, fsdp_size) + vec_shard.shape, vec_shard.dtype),
        ),
        in_specs=[pl.BlockSpec(memory_space=pltpu.VMEM)] * 2,
        out_specs=(pl.BlockSpec(memory_space=pltpu.VMEM),) * 2,
        scratch_shapes=[
            pltpu.SemaphoreType.DMA((sends,)),
            pltpu.SemaphoreType.DMA((3, dp_size, fsdp_size)),
            pltpu.SemaphoreType.DMA((3,)),
        ],
        compiler_params=pltpu.CompilerParams(
            collective_id=0, has_side_effects=True, vmem_limit_bytes=40 << 20
        ),
        name="gather_all",
    )(shard, vec_shard)


def reduce_kernel(
    dp_size,
    fsdp_size,
    big_ref,
    small_ref,
    big_out_ref,
    small_out_ref,
    big_near,
    small_near,
    big_sum,
    small_sum,
    big_dp,
    small_dp,
    big_part,
    small_part,
    big_z,
    small_z,
    big_end,
    small_end,
    send_sem,
    near_sem,
    dp_sem,
    z_sem,
    big_sem,
    small_sem,
    own_sem,
):
    depth = fsdp_size // 2
    me_dp, me_fsdp = lax.axis_index("dp"), lax.axis_index("fsdp")
    z, core = me_fsdp // 2, lax.rem(me_fsdp, 2)
    along_dp = [lax.rem(me_dp + i, dp_size) for i in range(1, dp_size)]
    along_z = [lax.rem(z + i, depth) for i in range(1, depth)]
    partner = (me_dp, z * 2 + 1 - core)
    dp_ids = [(other, me_fsdp) for other in along_dp]
    z_ids = [(me_dp, other * 2 + core) for other in along_z]
    meet([partner] + dp_ids + z_ids)
    started = []

    def push(held, target, semaphore, peer):
        copy = pltpu.make_async_remote_copy(
            src_ref=held,
            dst_ref=target,
            send_sem=send_sem.at[len(started)],
            recv_sem=semaphore,
            device_id=peer,
            device_id_type=MESH,
        )
        copy.start()
        started.append(copy)

    def arrived(block, semaphore):
        pltpu.make_async_remote_copy(
            src_ref=block,
            dst_ref=block,
            send_sem=send_sem.at[0],
            recv_sem=semaphore,
            device_id=partner,
            device_id_type=MESH,
        ).wait_recv()

    def wide(block):
        return block.astype(jnp.float32)

    for other in along_dp + [me_dp]:
        push(big_ref.at[1 - core, other], big_near.at[other], near_sem.at[0, other], partner)
        push(small_ref.at[1 - core, other], small_near.at[other], near_sem.at[1, other], partner)
    for other, peer in zip(along_dp, dp_ids):
        arrived(big_near.at[other], near_sem.at[0, other])
        arrived(small_near.at[other], near_sem.at[1, other])
        for level in range(depth):
            big_sum[other, level] = (
                wide(big_ref[core, other, level]) + wide(big_near[other, level])
            ).astype(big_sum.dtype)
            small_sum[other, level] = (
                wide(small_ref[core, other, level]) + wide(small_near[other, level])
            ).astype(small_sum.dtype)
        for level in range(depth):
            push(
                big_sum.at[other, level],
                big_dp.at[me_dp, level],
                dp_sem.at[0, me_dp, level],
                peer,
            )
            push(
                small_sum.at[other, level],
                small_dp.at[me_dp, level],
                dp_sem.at[1, me_dp, level],
                peer,
            )
    arrived(big_near.at[me_dp], near_sem.at[0, me_dp])
    arrived(small_near.at[me_dp], near_sem.at[1, me_dp])

    def over_dp(level):
        big = wide(big_ref[core, me_dp, level]) + wide(big_near[me_dp, level])
        small = wide(small_ref[core, me_dp, level]) + wide(small_near[me_dp, level])
        for other in along_dp:
            arrived(big_dp.at[other, level], dp_sem.at[0, other, level])
            arrived(small_dp.at[other, level], dp_sem.at[1, other, level])
            big = big + wide(big_dp[other, level])
            small = small + wide(small_dp[other, level])
        return big, small

    for level, peer in zip(along_z, z_ids):
        big, small = over_dp(level)
        big_part[level] = big.astype(big_part.dtype)
        small_part[level] = small.astype(small_part.dtype)
        push(big_part.at[level], big_z.at[z], z_sem.at[0, z], peer)
        push(small_part.at[level], small_z.at[z], z_sem.at[1, z], peer)
    big, small = over_dp(z)
    for level in along_z:
        arrived(small_z.at[level], z_sem.at[1, level])
        small = small + wide(small_z[level])
    small_end[...] = small.astype(small_end.dtype)
    for peer in z_ids + dp_ids + [partner]:
        push(small_end, small_out_ref.at[core, me_dp, z], small_sem.at[core, me_dp, z], peer)
    for level in along_z:
        arrived(big_z.at[level], z_sem.at[0, level])
        big = big + wide(big_z[level])
    big_end[...] = big.astype(big_end.dtype)
    for peer in dp_ids:
        push(big_end, big_out_ref.at[me_dp], big_sem.at[me_dp], peer)
    kept = [
        pltpu.make_async_copy(small_end, small_out_ref.at[core, me_dp, z], own_sem.at[0]),
        pltpu.make_async_copy(big_end, big_out_ref.at[me_dp], own_sem.at[1]),
    ]
    for copy in kept:
        copy.start()
    for level in along_z:
        block = small_out_ref.at[core, me_dp, level]
        arrived(block, small_sem.at[core, me_dp, level])
        for peer in dp_ids + [partner]:
            push(block, block, small_sem.at[core, me_dp, level], peer)
    for level in [z] + along_z:
        for other in along_dp:
            block = small_out_ref.at[core, other, level]
            arrived(block, small_sem.at[core, other, level])
            push(block, block, small_sem.at[core, other, level], partner)
    for other in along_dp:
        arrived(big_out_ref.at[other], big_sem.at[other])
    for level in [z] + along_z:
        for other in [me_dp] + along_dp:
            arrived(
                small_out_ref.at[1 - core, other, level], small_sem.at[1 - core, other, level]
            )
    for copy in kept:
        copy.wait()
    for copy in started:
        copy.wait_send()


def reduce_all(big, small, dp_size, fsdp_size):
    depth = fsdp_size // 2
    sends = 2 * dp_size + 2 * (dp_size - 1) * depth + 2 * (depth - 1)
    sends += (depth - 1) + dp_size + (dp_size - 1)
    sends += (depth - 1) * dp_size + depth * (dp_size - 1)
    shapes = (big.shape[3:], small.shape[3:])
    low = big.dtype
    scratch = []
    for lead in ((dp_size, depth), (dp_size, depth), (dp_size, depth), (depth,), (depth,), ()):
        scratch += [pltpu.VMEM(lead + shape, low) for shape in shapes]
    return pl.pallas_call(
        partial(reduce_kernel, dp_size, fsdp_size),
        out_shape=(
            jax.ShapeDtypeStruct((dp_size,) + shapes[0], low),
            jax.ShapeDtypeStruct(small.shape, low),
        ),
        in_specs=[pl.BlockSpec(memory_space=pltpu.VMEM)] * 2,
        out_specs=(pl.BlockSpec(memory_space=pltpu.VMEM),) * 2,
        scratch_shapes=scratch
        + [
            pltpu.SemaphoreType.DMA((sends,)),
            pltpu.SemaphoreType.DMA((2, dp_size)),
            pltpu.SemaphoreType.DMA((2, dp_size, depth)),
            pltpu.SemaphoreType.DMA((2, depth)),
            pltpu.SemaphoreType.DMA((dp_size,)),
            pltpu.SemaphoreType.DMA((2, dp_size, depth)),
            pltpu.SemaphoreType.DMA((2,)),
        ],
        compiler_params=pltpu.CompilerParams(
            collective_id=1, has_side_effects=True, vmem_limit_bytes=40 << 20
        ),
        name="reduce_all",
    )(big, small)


def scalar_kernel(
    dp_size, fsdp_size, part_ref, out_ref, row_slots, row_sum, dp_slots, send_sem, row_sem, dp_sem
):
    me_dp, me_fsdp = lax.axis_index("dp"), lax.axis_index("fsdp")
    along_dp = [lax.rem(me_dp + i, dp_size) for i in range(1, dp_size)]
    along_fsdp = [lax.rem(me_fsdp + i, fsdp_size) for i in range(1, fsdp_size)]
    meet([(me_dp, other) for other in along_fsdp] + [(other, me_fsdp) for other in along_dp])
    started = []

    def exchange(held, slots, semaphores, me, others, peers):
        for peer in peers:
            copy = pltpu.make_async_remote_copy(
                src_ref=held,
                dst_ref=slots.at[me],
                send_sem=send_sem.at[len(started)],
                recv_sem=semaphores.at[me],
                device_id=peer,
                device_id_type=MESH,
            )
            copy.start()
            started.append(copy)
        slots[me] = held[...]
        for other in others:
            pltpu.make_async_remote_copy(
                src_ref=held,
                dst_ref=slots.at[other],
                send_sem=send_sem.at[0],
                recv_sem=semaphores.at[other],
                device_id=peers[0],
                device_id_type=MESH,
            ).wait_recv()
        total = slots[0]
        for place in range(1, len(others) + 1):
            total = total + slots[place]
        return total

    row_sum[...] = exchange(
        part_ref, row_slots, row_sem, me_fsdp, along_fsdp, [(me_dp, other) for other in along_fsdp]
    )
    out_ref[...] = exchange(
        row_sum, dp_slots, dp_sem, me_dp, along_dp, [(other, me_fsdp) for other in along_dp]
    )
    for copy in started:
        copy.wait_send()


def scalar_sums(values, dp_size, fsdp_size):
    lanes = jnp.arange(128, dtype=jnp.int32)[None, :]
    tile = sum(jnp.where(lanes == index, value, 0.0) for index, value in enumerate(values))
    tile = jnp.broadcast_to(tile, (8, 128))
    sums = pl.pallas_call(
        partial(scalar_kernel, dp_size, fsdp_size),
        out_shape=jax.ShapeDtypeStruct((8, 128), jnp.float32),
        in_specs=[pl.BlockSpec(memory_space=pltpu.VMEM)],
        out_specs=pl.BlockSpec(memory_space=pltpu.VMEM),
        scratch_shapes=[
            pltpu.VMEM((fsdp_size, 8, 128), jnp.float32),
            pltpu.VMEM((8, 128), jnp.float32),
            pltpu.VMEM((dp_size, 8, 128), jnp.float32),
            pltpu.SemaphoreType.DMA((fsdp_size + dp_size,)),
            pltpu.SemaphoreType.DMA((fsdp_size,)),
            pltpu.SemaphoreType.DMA((dp_size,)),
        ],
        compiler_params=pltpu.CompilerParams(collective_id=2, has_side_effects=True),
        name="scalar_sums",
    )(tile)
    return [sums[0, index] for index in range(len(values))]


def three_parts(values):
    high = values.astype(jnp.bfloat16)
    rest = values - high.astype(jnp.float32)
    middle = rest.astype(jnp.bfloat16)
    return high, middle, (rest - middle.astype(jnp.float32)).astype(jnp.bfloat16)


def product(left, right, left_axis, right_axis):
    return lax.dot_general(
        left,
        right,
        (((left_axis,), (right_axis,)), ((), ())),
        preferred_element_type=jnp.float32,
    )


def local_step_kernel(
    chunk,
    embed_ref,
    head_ref,
    rows_ref,
    onehot_ref,
    target_ref,
    weight_ref,
    big_ref,
    taps_ref,
    wide_ref,
    loss_ref,
    inner_ref,
    first_ref,
    placed_ref,
    spread,
    tap_table,
    kept_third,
    kept_grad,
    sums,
):
    fsdp_size, inner, packed = weight_ref.shape
    width = embed_ref.shape[1]
    own = width // fsdp_size
    own_conv = packed - 2 * own
    slots = onehot_ref.shape[0]
    gain_one, bias_one = rows_ref[0:1, :], rows_ref[1:2, :]
    first_low = norm_gelu(embed_ref[...], gain_one, bias_one).astype(jnp.bfloat16)
    pre_inner = jnp.broadcast_to(rows_ref[6:7, :inner], (TABLE, inner))
    for row in range(fsdp_size):
        block = first_low[:, row * own : (row + 1) * own]
        first_ref[row] = block
        pre_inner = pre_inner + product(
            block, weight_ref[row, :, own_conv : own_conv + own], 1, 1
        )
    inner_ref[...] = pre_inner
    second_low = norm_gelu(pre_inner, rows_ref[5:6, :inner], rows_ref[5:6, inner:]).astype(
        jnp.bfloat16
    )
    spread[...] = jnp.zeros_like(spread)
    for tap in range(CONV_TAPS):
        spread[tap * TABLE : (tap + 1) * TABLE, tap * inner : (tap + 1) * inner] = second_low
    total = jnp.zeros((CONV_TAPS * TABLE, inner), jnp.float32)
    for row in range(fsdp_size):
        block = spread[:, row * own_conv : (row + 1) * own_conv]
        placed_ref[row] = block
        total = total + product(block, weight_ref[row, :, :own_conv], 1, 1)
    tap_table[...] = jnp.concatenate(three_parts(total), axis=1)
    sums[...] = jnp.zeros_like(sums)
    taps_ref[...] = jnp.zeros_like(taps_ref)
    wide_ref[...] = jnp.zeros_like(wide_ref)
    embed_low = embed_ref[...].astype(jnp.bfloat16)
    head = head_ref[...]
    gain_four, bias_four = rows_ref[3:4, :], rows_ref[4:5, :]

    def one_chunk(index, carry):
        here = pl.ds(pl.multiple_of(index * chunk, chunk), chunk)
        onehot = onehot_ref[here, :]
        centre = onehot[:, CONV_TAPS // 2 * TABLE : (CONV_TAPS // 2 + 1) * TABLE]
        parts = product(onehot, tap_table[...], 1, 0)
        conv_input = (
            parts[:, :inner]
            + parts[:, inner : 2 * inner]
            + parts[:, 2 * inner :]
            + rows_ref[6:7, inner:]
        )
        third_act, third_back = jax.vjp(
            norm_gelu, conv_input, rows_ref[7:8, :inner], rows_ref[7:8, inner:]
        )
        third_low = third_act.astype(jnp.bfloat16)
        kept_third[here, :] = third_low
        branch = jnp.concatenate(
            [
                product(third_low, weight_ref[row, :, own_conv + own :], 1, 0)
                for row in range(fsdp_size)
            ],
            axis=1,
        )
        summed = product(centre, embed_low, 1, 0) + branch + rows_ref[2:3, :]
        final, final_back = jax.vjp(layer_norm, summed, gain_four, bias_four)
        picked = final.astype(jnp.bfloat16)
        logits = product(picked, head, 1, 1)
        lanes = lax.broadcasted_iota(jnp.int32, logits.shape, 1)
        logits = jnp.where(lanes < VOCAB, logits, -1e30)
        target = target_ref[here, :]
        valid = target >= 0
        highest = jnp.max(logits, axis=1, keepdims=True)
        powers = jnp.exp(logits - highest)
        power_sum = jnp.sum(powers, axis=1, keepdims=True)
        hits = lanes == target
        chosen = jnp.sum(jnp.where(hits, logits, 0.0), axis=1, keepdims=True)
        losses = jnp.where(valid, jnp.log(power_sum) + highest - chosen, 0.0)
        logit_grad = jnp.where(valid, powers / power_sum - hits.astype(jnp.float32), 0.0).astype(
            jnp.bfloat16
        )
        picked_grad = product(logit_grad, head, 1, 0)
        sum_grad, gain_grad, bias_grad = final_back(picked_grad)
        branch_low = sum_grad.astype(jnp.bfloat16)
        kept_grad[here, :] = branch_low
        third_grad = jnp.zeros((chunk, inner), jnp.float32)
        for row in range(fsdp_size):
            third_grad = third_grad + product(
                branch_low[:, row * own : (row + 1) * own],
                weight_ref[row, :, own_conv + own :],
                1,
                1,
            )
        conv_pre, gain_three, bias_three = third_back(third_grad)
        taps_ref[...] += product(onehot, conv_pre.astype(jnp.bfloat16), 0, 0)
        high, middle, low = three_parts(sum_grad)
        wide_ref[0:TABLE, :] += (
            product(centre, high, 0, 0) + product(centre, middle, 0, 0) + product(centre, low, 0, 0)
        )
        wide_ref[TABLE : 2 * TABLE, :] += product(logit_grad, picked, 0, 0)
        wide_ref[2 * TABLE : 2 * TABLE + 1, :] += jnp.sum(
            branch_low.astype(jnp.float32), axis=0, keepdims=True
        )
        wide_ref[2 * TABLE + 1 : 2 * TABLE + 2, :] += gain_grad
        wide_ref[2 * TABLE + 2 : 2 * TABLE + 3, :] += bias_grad
        wide_ref[2 * TABLE + 3 : 2 * TABLE + 4, :inner] += gain_three
        wide_ref[2 * TABLE + 3 : 2 * TABLE + 4, inner:] += bias_three
        sums[0:1, :] += jnp.sum(jnp.broadcast_to(losses, (chunk, 128)), axis=0, keepdims=True)
        sums[1:2, :] += jnp.sum(
            jnp.broadcast_to(valid.astype(jnp.float32), (chunk, 128)), axis=0, keepdims=True
        )
        return carry

    lax.fori_loop(0, slots // chunk, one_chunk, 0)
    loss_ref[...] = sums[...]
    third_all = kept_third[...]

    for row in range(fsdp_size):
        big_ref[row] = product(
            kept_grad[:, row * own : (row + 1) * own], third_all, 0, 0
        ).astype(jnp.bfloat16)


def local_step(embed, head, rows, onehots, targets, weights):
    fsdp_size, inner, packed = weights.shape
    slots, width = onehots.shape[0], embed.shape[1]
    own = width // fsdp_size
    own_conv = packed - 2 * own
    shape = jax.ShapeDtypeStruct
    vmem = pl.BlockSpec(memory_space=pltpu.VMEM)
    return pl.pallas_call(
        partial(local_step_kernel, min(slots, 128)),
        out_shape=(
            shape((fsdp_size, own, inner), jnp.bfloat16),
            shape((CONV_TAPS * TABLE, inner), jnp.float32),
            shape((2 * TABLE + 8, width), jnp.float32),
            shape((8, 128), jnp.float32),
            shape((TABLE, inner), jnp.float32),
            shape((fsdp_size, TABLE, own), jnp.bfloat16),
            shape((fsdp_size, CONV_TAPS * TABLE, own_conv), jnp.bfloat16),
        ),
        in_specs=[vmem] * 6,
        out_specs=(vmem,) * 7,
        scratch_shapes=[
            pltpu.VMEM((CONV_TAPS * TABLE, CONV_TAPS * inner), jnp.bfloat16),
            pltpu.VMEM((CONV_TAPS * TABLE, 3 * inner), jnp.bfloat16),
            pltpu.VMEM((slots, inner), jnp.bfloat16),
            pltpu.VMEM((slots, width), jnp.bfloat16),
            pltpu.VMEM((8, 128), jnp.float32),
        ],
        compiler_params=pltpu.CompilerParams(vmem_limit_bytes=48 << 20),
        name="local_step",
    )(embed, head, rows, onehots, targets, weights)


def eigenbasis_update(
    gradient, master, moment, square, rotated_grads, col_start, first_correction, second_correction
):
    rotated = jnp.dot(gradient, rotated_grads, precision=highest_precision)
    moment_new = beta_one * moment + (1.0 - beta_one) * rotated
    square_new = beta_two * square + (1.0 - beta_two) * rotated * rotated
    step_ratio = (
        moment_new / first_correction / (jnp.sqrt(square_new / second_correction) + epsilon)
    )
    own_basis = lax.dynamic_slice_in_dim(rotated_grads, col_start, master.shape[1], 0)
    update = jnp.einsum("ri,ci->rc", step_ratio, own_basis, precision=highest_precision)
    master_new = master - rate_matrix * (update + decay_weight * master)
    return (master_new, master_new.astype(jnp.bfloat16), moment_new, square_new)


def adam_vectors(gradient, master, moment, square, first_correction, second_correction):
    decay_rows = jnp.where(
        jnp.arange(master.shape[0], dtype=jnp.int32)[:, None] < 2 * VOCAB, decay_weight, 0.0
    )
    moment_new = beta_one * moment + (1.0 - beta_one) * gradient
    square_new = beta_two * square + (1.0 - beta_two) * gradient * gradient
    step_ratio = (
        moment_new / first_correction / (jnp.sqrt(square_new / second_correction) + epsilon)
    )
    master_new = master - rate_vector * (step_ratio + decay_rows * master)
    return (master_new, master_new.astype(jnp.bfloat16), moment_new, square_new)


def local(
    input_tokens,
    item_numbers,
    loss_positions,
    target_tokens,
    input_projection,
    dilated_conv,
    output_projection,
    vectors,
    input_first_moment,
    input_second_moment,
    conv_first_moment,
    conv_second_moment,
    output_first_moment,
    output_second_moment,
    vector_first_moment,
    vector_second_moment,
    bases,
    eigenbasis_flags,
    optimizer_step,
):
    groups, col_index = lax.axis_size("dp"), lax.axis_index("dp")
    rows, row_index = lax.axis_size("fsdp"), lax.axis_index("fsdp")
    own_conv, own_in = dilated_conv.shape[0], input_projection.shape[0]
    shard = jnp.concatenate([dilated_conv, input_projection, output_projection], axis=0)
    all_weights, all_vectors = gather_all(
        shard.astype(jnp.bfloat16).T,
        vectors.astype(jnp.bfloat16).astype(jnp.float32).T,
        groups,
        rows,
    )

    width = own_in * rows
    inner = groups * input_projection.shape[1]
    start = 2 * VOCAB
    weights = all_weights.reshape(rows, inner, -1)
    table = all_vectors.reshape(width, -1).T
    spare = jnp.zeros((TABLE - VOCAB, width), jnp.float32)
    embedded = jnp.concatenate([table[:VOCAB], spare], axis=0)
    head = jnp.concatenate([table[VOCAB:start], spare], axis=0).astype(jnp.bfloat16)
    norm_rows = table[start:]
    onehots = tap_onehots(input_tokens, item_numbers, loss_positions)
    targets = jnp.where(loss_positions >= 0, target_tokens, -1).reshape(-1, 1)
    out_grad, tap_grads, wide_rows, loss_tile, pre_inner, first_low, placed = local_step(
        embedded, head, norm_rows, onehots.astype(jnp.bfloat16), targets, weights
    )
    summed_loss, slot_count = loss_tile[0, 0], loss_tile[1, 0]
    depth = rows // 2
    big = out_grad.reshape(depth, 2, groups, -1, inner)
    flat = jnp.concatenate(
        [tap_grads[:, at : at + 128] for at in range(0, inner, 128)]
        + [wide_rows[:, at : at + 128] for at in range(0, width, 128)],
        axis=0,
    )
    piece = -(-flat.shape[0] // (groups * rows * 16)) * 16
    padding = jnp.zeros((piece * groups * rows - flat.shape[0], 128), jnp.float32)
    small = jnp.concatenate([flat, padding], axis=0).astype(jnp.bfloat16)
    out_rows, small = reduce_all(
        big.transpose(1, 2, 0, 3, 4), small.reshape(2, groups, depth, piece, 128), groups, rows
    )
    out_rows = out_rows.reshape(-1, inner).astype(jnp.float32)
    small = small.reshape(-1, 128).astype(jnp.float32)
    taps = tap_grads.shape[0]
    tap_grads = jnp.concatenate(
        [small[at * taps : (at + 1) * taps] for at in range(inner // 128)], axis=1
    )
    small = small[taps * (inner // 128) :]
    count = wide_rows.shape[0]
    wide_rows = jnp.concatenate(
        [small[at * count : (at + 1) * count] for at in range(width // 128)], axis=1
    )

    weight_conv = weights[:, :, :own_conv].transpose(0, 2, 1).reshape(-1, inner)
    weight_in = weights[:, :, own_conv : own_conv + own_in].transpose(0, 2, 1).reshape(-1, inner)
    second_back = jax.vjp(norm_gelu, pre_inner, norm_rows[5, :inner], norm_rows[5, inner:])[1]
    first_back = jax.vjp(norm_gelu, embedded, norm_rows[0], norm_rows[1])[1]
    tap_view = tap_grads.reshape(CONV_TAPS, TABLE, inner)
    second_grad = sum(
        exact_dot(tap_view[tap], weight_conv[tap * inner : (tap + 1) * inner], (((1,), (1,)), ((), ())))
        for tap in range(CONV_TAPS)
    )
    inner_pre, gain_two, bias_two = second_back(second_grad)
    first_grad = exact_dot(inner_pre, weight_in, (((1,), (1,)), ((), ())))
    table_grad, gain_one, bias_one = first_back(first_grad)
    vec_sum = jnp.concatenate(
        [
            table_grad[:VOCAB] + wide_rows[:VOCAB],
            wide_rows[TABLE : TABLE + VOCAB],
            jnp.stack(
                [
                    gain_one,
                    bias_one,
                    wide_rows[2 * TABLE],
                    wide_rows[2 * TABLE + 1],
                    wide_rows[2 * TABLE + 2],
                    jnp.concatenate([gain_two, bias_two]),
                    jnp.concatenate(
                        [jnp.sum(inner_pre, axis=0), jnp.sum(tap_view[CONV_TAPS // 2], axis=0)]
                    ),
                    wide_rows[2 * TABLE + 3],
                ]
            ),
        ],
        axis=0,
    )
    own = width // (groups * rows)
    vec_own = lax.dynamic_slice_in_dim(vec_sum, (col_index * rows + row_index) * own, own, 1)

    row_low = lax.dynamic_index_in_dim(first_low, row_index, 0, False)
    in_rows = jnp.einsum(
        "vr,vi->ri", row_low.astype(jnp.float32), inner_pre, precision=highest_precision
    )
    placed_own = lax.dynamic_index_in_dim(placed, row_index, 0, False)
    conv_rows = jnp.einsum(
        "vr,vi->ri", placed_own.astype(jnp.float32), tap_grads, precision=highest_precision
    )

    col_width = input_projection.shape[1]
    col_start = col_index * col_width
    owned = [
        lax.dynamic_slice_in_dim(full_rows, col_start, col_width, 1)
        for full_rows in (in_rows, conv_rows, out_rows)
    ]
    square_local = sum((jnp.sum(piece * piece) for piece in owned)) + jnp.sum(vec_own * vec_own)
    square_total, summed_loss, slot_count = scalar_sums(
        (square_local, summed_loss, slot_count), groups, rows
    )
    grad_norm = jnp.sqrt(square_total) / slot_count
    factor = jnp.minimum(1.0, clip_limit / grad_norm) / slot_count
    step_value = optimizer_step[0].astype(jnp.float32)
    first_correction = 1.0 - beta_one**step_value
    second_correction = 1.0 - beta_two**step_value
    identity = jnp.eye(bases.shape[1], dtype=jnp.float32)
    rotated_grads = [
        jnp.where(eigenbasis_flags[mat_index] == 1, bases[mat_index], identity)
        for mat_index in range(3)
    ]
    master_in, copy_in, moment_in, square_in = eigenbasis_update(
        in_rows * factor,
        input_projection,
        input_first_moment,
        input_second_moment,
        rotated_grads[0],
        col_start,
        first_correction,
        second_correction,
    )
    updated_conv, conv_bfloat_copy, updated_conv_moment, updated_conv_square = eigenbasis_update(
        conv_rows * factor,
        dilated_conv,
        conv_first_moment,
        conv_second_moment,
        rotated_grads[1],
        col_start,
        first_correction,
        second_correction,
    )
    master_out, copy_out, moment_out, square_out = eigenbasis_update(
        out_rows * factor,
        output_projection,
        output_first_moment,
        output_second_moment,
        rotated_grads[2],
        col_start,
        first_correction,
        second_correction,
    )
    master_vec, copy_vec, moment_vec, square_vec = adam_vectors(
        vec_own * factor,
        vectors,
        vector_first_moment,
        vector_second_moment,
        first_correction,
        second_correction,
    )
    return (
        summed_loss / slot_count,
        grad_norm,
        master_in,
        copy_in,
        moment_in,
        square_in,
        updated_conv,
        conv_bfloat_copy,
        updated_conv_moment,
        updated_conv_square,
        master_out,
        copy_out,
        moment_out,
        square_out,
        master_vec,
        copy_vec,
        moment_vec,
        square_vec,
    )


def solution(mesh):
    placed = (
        P(None, ("dp", "fsdp")),
        P(None, ("dp", "fsdp")),
        P(None, ("dp", "fsdp")),
        P(None, ("dp", "fsdp")),
        P("fsdp", "dp"),
        P("fsdp", "dp"),
        P("fsdp", "dp"),
        P(None, ("dp", "fsdp")),
        P("fsdp", None),
        P("fsdp", None),
        P("fsdp", None),
        P("fsdp", None),
        P("fsdp", None),
        P("fsdp", None),
        P(None, ("dp", "fsdp")),
        P(None, ("dp", "fsdp")),
        P(),
        P(),
        P(),
    )
    return jax.shard_map(
        local,
        mesh=mesh,
        in_specs=placed,
        out_specs=(
            P(),
            P(),
            P("fsdp", "dp"),
            P("fsdp", "dp"),
            P("fsdp", None),
            P("fsdp", None),
            P("fsdp", "dp"),
            P("fsdp", "dp"),
            P("fsdp", None),
            P("fsdp", None),
            P("fsdp", "dp"),
            P("fsdp", "dp"),
            P("fsdp", None),
            P("fsdp", None),
            P(None, ("dp", "fsdp")),
            P(None, ("dp", "fsdp")),
            P(None, ("dp", "fsdp")),
            P(None, ("dp", "fsdp")),
        ),
        check_vma=False,
    )
```

profile of v0, /device:TPU:0, one launch (start us, length us, event | category | flops | bytes accessed | tf_op | source)
XLA Modules:
  0.0 210.3 jit_solution(7613127158968134621)
XLA Ops:
  0.7 0.8 reshape.234
  1.5 0.8 reshape.235
  2.5 0.5 select_reduce_fusion.1
  3.6 0.2 concatenate.69
  4.3 51.9 %gather_all.1 = (bf16[8,4,160,720]{3,2,1,0:T(8,128)(2,1)S(1)}, f32[4,8,40,68]{3,2,1,0:T(8,128)S(1)}) custom-call(bf16[160,720]{1,0:T(8,128)(2,1)S(1)} %maximum_bitcast_fusion.shard_ref, f32[40,68]{1,0:T(8,128)S(1)} %convert_bitcast_fusion.vec_ref), custom_call_target="tpu_custom_call" | custom-call | tf_op jit(solution)/shard_map/gather_all/pallas_call | solution.py:210
  56.2 3.1 %copy-done = bf16[8,4,160,720]{3,2,1,0:T(8,128)(2,1)} copy-done((bf16[8,4,160,720]{3,2,1,0:T(8,128)(2,1)}, bf16[8,4,160,720]{3,2,1,0:T(8,128)(2,1)S(1)}, u32[]{:S(2)}) %copy-start) | copy-done | bytes 7372824
  59.3 0.2 copy.65
  60.2 18.0 %local_step.1 = (bf16[8,160,640]{2,1,0:T(8,128)(2,1)S(1)}, f32[160,640]{1,0:T(8,128)S(1)}, f32[72,1280]{1,0:T(8,128)S(1)}, f32[8,128]{1,0:T(8,128)S(1)}, f32[32,...) custom-call(f32[32,1280]{1,0:T(8,128)S(1)} %get-tuple-element.133.embed_ref, ...), custom_call_target="tpu_custom_call" | custom-call | tf_op jit(solution)/shard_map/local_step/pallas_call | solution.py:644
  78.6 39.2 %reduce_all.1 = (bf16[4,40,640]{2,1,0:T(8,128)(2,1)S(1)}, bf16[2,4,4,48,128]{4,3,2,1,0:T(8,128)(2,1)S(1)}) custom-call(bf16[2,4,4,40,640]{4,3,2,1,0:T(8,128)(2,1)S(1)} %bitcast.75, bf16[2,4,4,48,128]{4,3,2,1,0:T(8,128)(2,1)S(1)} %bitcast.78), custom_call_target="tpu_custom_call" | custom-call | tf_op jit(solution)/shard_map/reduce_all/pallas_call | solution.py:390
  118.1 0.8 copy-done.4
  118.9 2.8 %slice_bitcast_fusion = bf16[8,400,640]{1,2,0:T(8,128)(2,1)} fusion(bf16[8,640,720]{2,1,0:T(8,128)(2,1)S(1)} %bitcast.74), kind=kLoop, calls=%fused_computation | loop fusion | bytes 8192000 | tf_op jit(solution)/shard_map/transpose | solution.py:769
  121.6 7.5 %copy.68 = bf16[8,400,640]{2,1,0:T(8,128)(2,1)} copy(bf16[8,400,640]{1,2,0:T(8,128)(2,1)} %slice_bitcast_fusion) | data formatting | bytes 8192000 | tf_op jit(solution)/shard_map/transpose | solution.py:769
  129.2 1.6 fusion.26
  130.8 1.5 fusion.29
  132.3 1.5 fusion.32
  133.8 1.5 fusion.35
  135.4 1.5 fusion.38
  136.9 0.4 convolution_add_fusion.8
  137.3 0.4 fusion.15
  137.6 0.4 fusion.14
  138.0 0.4 fusion.13
  138.8 1.6 multiply_reduce_fusion.6
  140.8 5.0 %slice_bitcast_fusion.1 = bf16[8,160,640]{1,2,0:T(8,128)(2,1)} fusion(bf16[8,640,720]{2,1,0:T(8,128)(2,1)} %bitcast.71), kind=kLoop, calls=%fused_computation.1 | loop fusion | bytes 3276800 | tf_op jit(solution)/shard_map/transpose | solution.py:770
  145.8 3.0 %copy.69 = bf16[8,160,640]{2,1,0:T(8,128)(2,1)S(1)} copy(bf16[8,160,640]{1,2,0:T(8,128)(2,1)} %slice_bitcast_fusion.1) | data formatting | bytes 3276800 | tf_op jit(solution)/shard_map/transpose | solution.py:770
  148.8 0.6 fusion.88
  149.4 0.4 copy-done.6
  149.8 0.7 multiply_reduce_fusion.1
  150.8 0.8 constant_dynamic-update-slice_fusion.25
  151.6 0.8 constant_dynamic-update-slice_fusion.24
  152.4 0.8 constant_dynamic-update-slice_fusion.23
  153.1 0.8 constant_dynamic-update-slice_fusion.22
  153.9 0.8 constant_dynamic-update-slice_fusion.21
  154.7 0.8 constant_dynamic-update-slice_fusion.20
  155.5 0.8 constant_dynamic-update-slice_fusion.19
  156.2 0.8 constant_dynamic-update-slice_fusion.18
  157.0 0.8 constant_dynamic-update-slice_fusion.17
  157.8 0.8 constant_dynamic-update-slice_fusion.16
  158.7 0.4 concatenate.75
  159.1 0.7 multiply_reduce_fusion.9
  159.8 0.7 fusion.75
  160.5 0.8 multiply_reduce_fusion
  161.3 0.4 fusion.86
  161.7 0.7 multiply_reduce_fusion.5
  163.8 0.7 multiply_reduce_fusion.4
  165.8 0.5 fusion.123
  166.3 1.3 fusion.106
  167.6 0.6 broadcast_in_dim.99.part_ref
  168.2 10.4 %scalar_sums.1 = f32[8,128]{1,0:T(8,128)} custom-call(f32[8,128]{1,0:T(8,128)} %broadcast_in_dim.99.part_ref), custom_call_target="tpu_custom_call" | custom-call | tf_op jit(solution)/shard_map/scalar_sums/pallas_call | solution.py:465
  178.6 1.4 fusion.122
  183.1 1.0 fusion.113
  184.1 0.7 copy.75
  184.8 0.7 copy.77
  185.5 0.7 copy.78
  186.2 0.7 copy.76
  186.9 0.6 fusion.124
  188.1 3.0 %fusion.45 = (f32[160,640]{1,0:T(8,128)S(1)}, f32[160,640]{1,0:T(8,128)S(1)}) fusion(f32[160,640]{1,0:T(8,128)S(1)} %copy-done.12, f32[160,640]{1,0:T(8,128)} %param.31, f32[160,640]{1,0:T(8,128)S(1)} %bitcast.101, f32[3,640,640]{2,1,0:T(8,128)} %param.35, pred[]{:T(512)} %bitcast.35), kind=kOutput, calls=%fused_computation.66 | convolution fusion | flops 788377600 | bytes 3686912 | tf_op jit(solution)/shard_map/dot_general | solution.py:672
  191.3 1.9 slice_bitcast_fusion.2
  193.2 1.4 fusion.127
  196.2 1.0 copy-done.7
  197.2 0.3 copy-done.8
  197.5 3.2 %fusion.16 = (f32[400,640]{1,0:T(8,128)S(1)}, f32[400,640]{1,0:T(8,128)S(1)}) fusion(f32[400,640]{1,0:T(8,128)S(1)} %copy-done.7, f32[400,640]{1,0:T(8,128)S(1)} %copy-done.8, f32[640,640]{1,0:T(8,128)S(1)} %get-tuple-element.124, f32[400,640]{1,0:T(8,128)S(1)} %fusion.75, f32[]{:T(128)S(6)} %div.109), kind=kOutput, calls=%fused_computation.34 | convolution fusion | flops 1968128000 | bytes 6758404 | tf_op jit(solution)/shard_map/dot_general | solution.py:672
  200.7 2.4 %fusion.126 = (bf16[400,160]{0,1:T(8,128)(2,1)}, f32[400,160]{0,1:T(8,128)}) fusion(f32[400,160]{0,1:T(8,128)S(1)} %copy-done.20, f32[640,640]{1,0:T(8,128)S(1)} %get-tuple-element.124, s32[]{:T(128)S(6)} %select_n.150, f32[400,640]{1,0:T(8,128)S(1)} %get-tuple-element.127, f32[400,640]{1,0:T(8,128)S(1)} %get-tuple-element.126, f32[]{:T(128)} %bitcast.31, ...), kind=kOutput, calls=%fused_computation.263 | convolution fusion | flops 492864000 | bytes 3169292 | tf_op jit(solution)/shard_map/ri,ci->rc/dot_general | solution.py:679
  203.2 1.4 fusion.44
  204.6 1.4 fusion.125
  (150 shorter events, 4.0 us)
Async XLA Ops:
  0.7 1.8 copy-start.30
  0.7 1.8 copy-start.31
  2.3 1.5 copy-start.19
  2.4 1.5 copy-start.23
  2.4 1.6 copy-start.21
  2.5 1.8 copy-start.25
  3.6 56.0 %copy-start.28 = (pred[32]{0:T(512)(128)(4,1)S(1)}, pred[32]{0:T(512)(128)(4,1)}, u32[]{:S(2)}) copy-start(pred[32]{0:T(512)(128)(4,1)} %constant.37.clone.1) | copy-start | bytes 100
  56.2 3.1 %copy-start = (bf16[8,4,160,720]{3,2,1,0:T(8,128)(2,1)}, bf16[8,4,160,720]{3,2,1,0:T(8,128)(2,1)S(1)}, u32[]{:S(2)}) copy-start(bf16[8,4,160,720]{3,2,1,0:T(8,128)(2,1)S(1)} %get-tuple-element.30) | copy-start | bytes 22118404
  59.5 79.2 %copy-start.5 = (f32[1280,68]{0,1:T(8,128)}, f32[1280,68]{0,1:T(8,128)S(1)}, u32[]{:S(2)}) copy-start(f32[1280,68]{0,1:T(8,128)S(1)} %copy.65) | copy-start | bytes 1044484
  60.2 58.7 %slice-start = ((s8[7864320]{0:T(1024)(128)(4,1)}), s8[3670016]{0:T(1024)(128)(4,1)S(1)}, s32[]{:S(2)}) async-start(s8[7864320]{0:T(1024)(128)(4,1)} %bitcast.72), calls=%async_computation | async-start | bytes 7340032
  78.2 40.7 %slice-start.1 = ((s8[7864320]{0:T(1024)(128)(4,1)}), s8[4194304]{0:T(1024)(128)(4,1)S(1)}, s32[]{:S(2)}) async-start(s8[7864320]{0:T(1024)(128)(4,1)} %bitcast.72), calls=%async_computation.1 | async-start | bytes 8388608
  118.0 0.9 copy-start.4
  118.9 21.9 %copy-start.2 = (f32[160,640]{1,0:T(8,128)}, f32[160,640]{1,0:T(8,128)S(1)}, u32[]{:S(2)}) copy-start(f32[160,640]{1,0:T(8,128)S(1)} %slice_dynamic-update-slice_fusion) | copy-start | bytes 1228804
  129.2 7.7 %copy-start.1 = (bf16[8,400,640]{2,1,0:T(8,128)(2,1)S(1)}, bf16[8,400,640]{2,1,0:T(8,128)(2,1)}, u32[]{:S(2)}) copy-start(bf16[8,400,640]{2,1,0:T(8,128)(2,1)} %copy.68) | copy-start | bytes 12288004
  148.8 1.0 copy-start.6
  150.6 9.2 %copy-start.3 = (f32[160,640]{1,0:T(8,128)S(1)}, f32[160,640]{1,0:T(8,128)}, u32[]{:S(2)}) copy-start(f32[160,640]{1,0:T(8,128)} %copy-done.2) | copy-start | bytes 1228804
  159.1 0.7 copy-start.11
  159.8 23.0 %copy-start.26 = (f32[68,40]{0,1:T(8,128)S(1)}, f32[68,40]{0,1:T(8,128)}, u32[]{:S(2)}) copy-start(f32[68,40]{0,1:T(8,128)} %param.33) | copy-start | bytes 32644
  159.8 23.1 %copy-start.27 = (f32[68,40]{0,1:T(8,128)S(1)}, f32[68,40]{0,1:T(8,128)}, u32[]{:S(2)}) copy-start(f32[68,40]{0,1:T(8,128)} %param.34) | copy-start | bytes 32644
  160.5 26.4 %copy-start.29 = (s32[3]{0:T(128)S(1)}, s32[3]{0:T(128)}, u32[]{:S(2)}) copy-start(s32[3]{0:T(128)} %param.36) | copy-start | bytes 40
  160.5 27.6 %copy-start.12 = (f32[160,640]{1,0:T(8,128)S(1)}, f32[160,640]{1,0:T(8,128)}, u32[]{:S(2)}) copy-start(f32[160,640]{1,0:T(8,128)} %param.32) | copy-start | bytes 1228804
  163.7 32.2 %slice-start.2 = ((s8[4915200]{0:T(1024)(128)(4,1)}), s8[720896]{0:T(1024)(128)(4,1)S(1)}, s32[]{:S(2)}) async-start(s8[4915200]{0:T(1024)(128)(4,1)} %bitcast.89), calls=%async_computation.2 | async-start | bytes 1441792
  191.1 2.1 copy-start.15
  191.1 2.1 copy-start.16
  191.1 4.8 %slice-start.3 = ((s8[4915200]{0:T(1024)(128)(4,1)}), s8[4194304]{0:T(1024)(128)(4,1)S(1)}, s32[]{:S(2)}) async-start(s8[4915200]{0:T(1024)(128)(4,1)} %bitcast.89), calls=%async_computation.3 | async-start | bytes 8388608
  191.3 2.0 copy-start.22
  196.0 1.2 copy-start.7
  196.0 1.5 copy-start.8
  197.5 3.2 %copy-start.20 = (f32[400,160]{0,1:T(8,128)S(1)}, f32[400,160]{0,1:T(8,128)}, u32[]{:S(2)}) copy-start(f32[400,160]{0,1:T(8,128)} %param.24) | copy-start | bytes 768004
  200.7 2.5 %copy-start.9 = (f32[400,640]{1,0:T(8,128)}, f32[400,640]{1,0:T(8,128)S(1)}, u32[]{:S(2)}) copy-start(f32[400,640]{1,0:T(8,128)S(1)} %get-tuple-element.126) | copy-start | bytes 3072004
  200.7 2.5 %copy-start.10 = (f32[400,640]{1,0:T(8,128)}, f32[400,640]{1,0:T(8,128)S(1)}, u32[]{:S(2)}) copy-start(f32[400,640]{1,0:T(8,128)S(1)} %get-tuple-element.127) | copy-start | bytes 3072004
  200.7 2.4 %copy-start.13 = (f32[160,640]{1,0:T(8,128)S(1)}, f32[160,640]{1,0:T(8,128)}, u32[]{:S(2)}) copy-start(f32[160,640]{1,0:T(8,128)} %param.28) | copy-start | bytes 1228804
  200.7 2.4 %copy-start.14 = (f32[160,640]{1,0:T(8,128)S(1)}, f32[160,640]{1,0:T(8,128)}, u32[]{:S(2)}) copy-start(f32[160,640]{1,0:T(8,128)} %param.27) | copy-start | bytes 1228804
  203.2 1.5 copy-start.24
  204.6 1.5 copy-start.17
  204.6 1.5 copy-start.18
where the time goes:
time: 212 us; the launch traced here: 210 us
  Pallas kernels  120 us (57%)
  local copies, waits for them, and re-layouts  43.1 us (20%)
  matrix products  25.9 us (12%)
  between operations  13.3 us (6%)
  other arithmetic  8.36 us (4%)
    pallas_call x1, Pallas kernels, gather_all(): pl.pallas_call(partial(gather_kernel, dp_size, fsdp_size, cut), out_shape...  51.9 us
    pallas_call x1, Pallas kernels, reduce_all(): pl.pallas_call(partial(reduce_kernel, dp_size, fsdp_size), out_shape=(jax...  39.2 us
    pallas_call x1, Pallas kernels, local_step(): pl.pallas_call(partial(local_step_kernel, min(slots, 128)), out_shape=(sh...  18 us
    unnamed x109, local copies, waits for them, and re-layouts  16.1 us
    pallas_call x1, Pallas kernels, scalar_sums(): pl.pallas_call(partial(scalar_kernel, dp_size, fsdp_size), out_shape=jax....  10.4 us
    transpose x2, local copies, waits for them, and re-layouts, local(): weight_conv = weights[:, :, :own_conv].transpose(0, 2, 1).reshape(-1, inner)  10.3 us
    dot_general x6, matrix products, exact_dot(): lax.dot_general(high, right, contract, preferred_element_type=jnp.float32)  8.23 us
    transpose x2, local copies, waits for them, and re-layouts, local(): weights[:, :, own_conv:own_conv + own_in].transpose(0, 2, 1)  7.98 us

commit v1 on v0

--- a/solution.py
+++ b/solution.py
@@ -1,3 +1,4 @@
+import math
 from functools import partial
 
 import jax
@@ -61,18 +62,6 @@
         keep = valid & (item == own_item) & (own_item >= 0)
         result.append(jnp.where(keep, token, -1)[:, :, None] == identities)
     return jnp.concatenate(result, axis=2).reshape(batches * slots, CONV_TAPS * TABLE)
-
-
-def exact_dot(left, right, contract):
-    high = left.astype(jnp.bfloat16)
-    low = (left - high.astype(jnp.float32)).astype(jnp.bfloat16)
-    return lax.dot_general(high, right, contract, preferred_element_type=jnp.float32) + lax.dot_general(
-        low, right, contract, preferred_element_type=jnp.float32
-    )
-
-
-def column_sum(values):
-    return jnp.sum(values, axis=0, dtype=jnp.float32)
 
 
 def split_two(count):
@@ -221,7 +210,7 @@
             pltpu.SemaphoreType.DMA((3,)),
         ],
         compiler_params=pltpu.CompilerParams(
-            collective_id=0, has_side_effects=True, vmem_limit_bytes=40 << 20
+            collective_id=0, has_side_effects=True, vmem_limit_bytes=20 << 20
         ),
         name="gather_all",
     )(shard, vec_shard)
@@ -406,7 +395,7 @@
             pltpu.SemaphoreType.DMA((2,)),
         ],
         compiler_params=pltpu.CompilerParams(
-            collective_id=1, has_side_effects=True, vmem_limit_bytes=40 << 20
+            collective_id=1, has_side_effects=True, vmem_limit_bytes=20 << 20
         ),
         name="reduce_all",
     )(big, small)
@@ -458,11 +447,8 @@
         copy.wait_send()
 
 
-def scalar_sums(values, dp_size, fsdp_size):
-    lanes = jnp.arange(128, dtype=jnp.int32)[None, :]
-    tile = sum(jnp.where(lanes == index, value, 0.0) for index, value in enumerate(values))
-    tile = jnp.broadcast_to(tile, (8, 128))
-    sums = pl.pallas_call(
+def scalar_sums(tile, dp_size, fsdp_size):
+    return pl.pallas_call(
         partial(scalar_kernel, dp_size, fsdp_size),
         out_shape=jax.ShapeDtypeStruct((8, 128), jnp.float32),
         in_specs=[pl.BlockSpec(memory_space=pltpu.VMEM)],
@@ -475,10 +461,9 @@
             pltpu.SemaphoreType.DMA((fsdp_size,)),
             pltpu.SemaphoreType.DMA((dp_size,)),
         ],
-        compiler_params=pltpu.CompilerParams(collective_id=2, has_side_effects=True),
+        compiler_params=pltpu.CompilerParams(collective_id=2, has_side_effects=True, vmem_limit_bytes=4 << 20),
         name="scalar_sums",
     )(tile)
-    return [sums[0, index] for index in range(len(values))]
 
 
 def three_parts(values):
@@ -661,24 +646,237 @@
             pltpu.VMEM((slots, width), jnp.bfloat16),
             pltpu.VMEM((8, 128), jnp.float32),
         ],
-        compiler_params=pltpu.CompilerParams(vmem_limit_bytes=48 << 20),
+        compiler_params=pltpu.CompilerParams(vmem_limit_bytes=28 << 20),
         name="local_step",
     )(embed, head, rows, onehots, targets, weights)
 
 
-def eigenbasis_update(
-    gradient, master, moment, square, rotated_grads, col_start, first_correction, second_correction
+def table_step_kernel(
+    small_ref,
+    embed_ref,
+    rows_ref,
+    weight_ref,
+    inner_ref,
+    first_ref,
+    placed_ref,
+    out_rows_ref,
+    in_rows_ref,
+    conv_rows_ref,
+    vec_ref,
+    square_ref,
 ):
-    rotated = jnp.dot(gradient, rotated_grads, precision=highest_precision)
-    moment_new = beta_one * moment + (1.0 - beta_one) * rotated
-    square_new = beta_two * square + (1.0 - beta_two) * rotated * rotated
-    step_ratio = (
-        moment_new / first_correction / (jnp.sqrt(square_new / second_correction) + epsilon)
-    )
-    own_basis = lax.dynamic_slice_in_dim(rotated_grads, col_start, master.shape[1], 0)
-    update = jnp.einsum("ri,ci->rc", step_ratio, own_basis, precision=highest_precision)
-    master_new = master - rate_matrix * (update + decay_weight * master)
-    return (master_new, master_new.astype(jnp.bfloat16), moment_new, square_new)
+    fsdp_size, inner, packed = weight_ref.shape
+    width = embed_ref.shape[1]
+    own = width // fsdp_size
+    own_conv = packed - 2 * own
+    me_dp, me_fsdp = lax.axis_index("dp"), lax.axis_index("fsdp")
+    tap_rows = CONV_TAPS * TABLE
+    wide_count = 2 * TABLE + 8
+    small = small_ref[...].astype(jnp.float32)
+    taps = jnp.concatenate(
+        [small[at * tap_rows : (at + 1) * tap_rows] for at in range(inner // 128)], axis=1
+    )
+    begin = tap_rows * (inner // 128)
+    wide = jnp.concatenate(
+        [
+            small[begin + at * wide_count : begin + (at + 1) * wide_count]
+            for at in range(width // 128)
+        ],
+        axis=1,
+    )
+    conv_rows_ref[...] = product(placed_ref[me_fsdp], taps.astype(jnp.bfloat16), 0, 0)
+    taps_low = taps.astype(jnp.bfloat16)
+    columns = jnp.concatenate(
+        [
+            product(taps_low, weight_ref[row, :, :own_conv], 1, 0)
+            for row in range(fsdp_size)
+        ],
+        axis=1,
+    )
+    second_grad = jnp.zeros((TABLE, inner), jnp.float32)
+    for tap in range(CONV_TAPS):
+        second_grad = second_grad + columns[
+            tap * TABLE : (tap + 1) * TABLE, tap * inner : (tap + 1) * inner
+        ]
+    second_back = jax.vjp(
+        norm_gelu, inner_ref[...], rows_ref[5:6, :inner], rows_ref[5:6, inner:]
+    )[1]
+    inner_pre, gain_two, bias_two = second_back(second_grad)
+    high, middle, low = three_parts(inner_pre)
+    first_own = first_ref[me_fsdp]
+    in_rows_ref[...] = (
+        product(first_own, high, 0, 0) + product(first_own, middle, 0, 0) + product(first_own, low, 0, 0)
+    )
+    stacked = jnp.concatenate([high, middle], axis=0)
+    pieces = []
+    for row in range(fsdp_size):
+        piece = product(stacked, weight_ref[row, :, own_conv : own_conv + own], 1, 0)
+        pieces.append(piece[:TABLE] + piece[TABLE:])
+    first_back = jax.vjp(norm_gelu, embed_ref[...], rows_ref[0:1, :], rows_ref[1:2, :])[1]
+    table_grad, gain_one, bias_one = first_back(jnp.concatenate(pieces, axis=1))
+    centre = CONV_TAPS // 2 * TABLE
+    vec_ref[0:TABLE, :] = table_grad + wide[0:TABLE]
+    vec_ref[TABLE : 2 * TABLE, :] = wide[TABLE : 2 * TABLE]
+    vec_ref[2 * TABLE : 2 * TABLE + 1, :] = gain_one
+    vec_ref[2 * TABLE + 1 : 2 * TABLE + 2, :] = bias_one
+    vec_ref[2 * TABLE + 2 : 2 * TABLE + 5, :] = wide[2 * TABLE : 2 * TABLE + 3]
+    vec_ref[2 * TABLE + 5 : 2 * TABLE + 6, :inner] = gain_two
+    vec_ref[2 * TABLE + 5 : 2 * TABLE + 6, inner:] = bias_two
+    vec_ref[2 * TABLE + 6 : 2 * TABLE + 7, :inner] = jnp.sum(inner_pre, axis=0, keepdims=True)
+    vec_ref[2 * TABLE + 6 : 2 * TABLE + 7, inner:] = jnp.sum(
+        taps[centre : centre + TABLE], axis=0, keepdims=True
+    )
+    vec_ref[2 * TABLE + 7 : 2 * TABLE + 8, :] = wide[2 * TABLE + 3 : 2 * TABLE + 4]
+
+    def squares(values, group, block):
+        lanes = lax.broadcasted_iota(jnp.int32, values.shape, 1)
+        mine = (lanes >= group * block) & (lanes < (group + 1) * block)
+        kept = jnp.where(mine, values, 0.0)
+        rows = jnp.sum(kept * kept, axis=0, keepdims=True)
+        return jnp.sum(rows, axis=1, keepdims=True)
+
+    groups = lax.axis_size("dp")
+    block = inner // groups
+    total = squares(in_rows_ref[...], me_dp, block)
+    total = total + squares(conv_rows_ref[...], me_dp, block)
+    total = total + squares(out_rows_ref[...].astype(jnp.float32), me_dp, block)
+    vec_block = width // (groups * fsdp_size)
+    total = total + squares(vec_ref[...], me_dp * fsdp_size + me_fsdp, vec_block)
+    square_ref[...] = jnp.broadcast_to(total, square_ref.shape)
+
+
+def table_step(small, embed, rows, weights, pre_inner, first_low, placed, out_rows):
+    fsdp_size, inner, packed = weights.shape
+    width = embed.shape[1]
+    own = width // fsdp_size
+    shape = jax.ShapeDtypeStruct
+    vmem = pl.BlockSpec(memory_space=pltpu.VMEM)
+    return pl.pallas_call(
+        table_step_kernel,
+        out_shape=(
+            shape((own, inner), jnp.float32),
+            shape((packed - 2 * own, inner), jnp.float32),
+            shape((2 * TABLE + 8, width), jnp.float32),
+            shape((8, 128), jnp.float32),
+        ),
+        in_specs=[vmem] * 8,
+        out_specs=(vmem,) * 4,
+        compiler_params=pltpu.CompilerParams(vmem_limit_bytes=28 << 20),
+        name="table_step",
+    )(small, embed, rows, weights, pre_inner, first_low, placed, out_rows)
+
+
+def precise(left, right, left_axis, right_axis):
+    return lax.dot_general(
+        left,
+        right,
+        (((left_axis,), (right_axis,)), ((), ())),
+        precision=highest_precision,
+        preferred_element_type=jnp.float32,
+    )
+
+
+def update_kernel(index, transposed, *refs):
+    (
+        flag_ref,
+        step_ref,
+        sums_ref,
+        grad_ref,
+        base_ref,
+        master_ref,
+        moment_ref,
+        square_ref,
+        master_out,
+        copy_out,
+        moment_out,
+        square_out,
+        rotated,
+    ) = refs
+    count = sums_ref[2:3, 0:1]
+    grad_norm = jnp.sqrt(sums_ref[0:1, 0:1]) / count
+    factor = jnp.minimum(1.0, clip_limit / grad_norm) / count
+    first_correction, second_correction = corrections(step_ref[0])
+    turned = flag_ref[index] == 1
+
+    @pl.when(turned)
+    def _():
+        rotated[...] = precise(grad_ref[...].astype(jnp.float32), base_ref[0], 1, 0)
+
+    @pl.when(jnp.logical_not(turned))
+    def _():
+        rotated[...] = grad_ref[...].astype(jnp.float32)
+
+    chunk = 40
+
+    def one_chunk(step, carry):
+        here = pl.ds(pl.multiple_of(step * chunk, 8), chunk)
+        value = rotated[here, :] * factor
+        moment = beta_one * moment_ref[here, :] + (1.0 - beta_one) * value
+        square = beta_two * square_ref[here, :] + (1.0 - beta_two) * value * value
+        moment_out[here, :] = moment
+        square_out[here, :] = square
+        rotated[here, :] = (
+            moment / first_correction / (jnp.sqrt(square / second_correction) + epsilon)
+        )
+        return carry
+
+    lax.fori_loop(0, rotated.shape[0] // chunk, one_chunk, 0)
+    width = master_ref.shape[0] if transposed else master_ref.shape[1]
+    start = lax.axis_index("dp") * width
+
+    def finish(update):
+        master = master_ref[...]
+        master = master - rate_matrix * (update + decay_weight * master)
+        master_out[...] = master
+        copy_out[...] = master.astype(jnp.bfloat16)
+
+    own_rows = pl.ds(pl.multiple_of(start, 8), width)
+
+    @pl.when(turned)
+    def _():
+        if transposed:
+            finish(precise(base_ref[0, own_rows, :], rotated[...], 1, 1))
+        else:
+            finish(precise(rotated[...], base_ref[0, own_rows, :], 1, 1))
+
+    @pl.when(jnp.logical_not(turned))
+    def _():
+        inner = rotated.shape[1]
+        rows = lax.broadcasted_iota(jnp.int32, (width, inner), 0) + start
+        picks = (rows == lax.broadcasted_iota(jnp.int32, (width, inner), 1)).astype(jnp.float32)
+        if transposed:
+            finish(precise(picks, rotated[...], 1, 1))
+        else:
+            finish(precise(rotated[...], picks, 1, 1))
+
+
+def corrections(step):
+    value = jnp.full((1, 1), step.astype(jnp.float32))
+    return 1.0 - jnp.exp(value * math.log(beta_one)), 1.0 - jnp.exp(value * math.log(beta_two))
+
+
+def matrix_update(index, transposed, flags, step, sums, gradient, bases, master, moment, square):
+    inner = moment.shape[1]
+    shape = jax.ShapeDtypeStruct
+    vmem = pl.BlockSpec(memory_space=pltpu.VMEM)
+    smem = pl.BlockSpec(memory_space=pltpu.SMEM)
+    return pl.pallas_call(
+        partial(update_kernel, index, transposed),
+        grid=(1,),
+        out_shape=(
+            shape(master.shape, jnp.float32),
+            shape(master.shape, jnp.bfloat16),
+            shape(moment.shape, jnp.float32),
+            shape(moment.shape, jnp.float32),
+        ),
+        in_specs=[smem, smem, vmem, vmem]
+        + [pl.BlockSpec((1, inner, inner), lambda at: (index, 0, 0))]
+        + [vmem] * 3,
+        out_specs=(vmem,) * 4,
+        scratch_shapes=[pltpu.VMEM(moment.shape, jnp.float32)],
+        compiler_params=pltpu.CompilerParams(vmem_limit_bytes=28 << 20),
+        name="update_%d" % index,
+    )(flags, step, sums, gradient, bases, master, moment, square)
 
 
 def adam_vectors(gradient, master, moment, square, first_correction, second_correction):
@@ -721,7 +919,7 @@
     shard = jnp.concatenate([dilated_conv, input_projection, output_projection], axis=0)
     all_weights, all_vectors = gather_all(
         shard.astype(jnp.bfloat16).T,
-        vectors.astype(jnp.bfloat16).astype(jnp.float32).T,
+        lax.reduce_precision(vectors, 8, 7).T,
         groups,
         rows,
     )
@@ -740,7 +938,6 @@
     out_grad, tap_grads, wide_rows, loss_tile, pre_inner, first_low, placed = local_step(
         embedded, head, norm_rows, onehots.astype(jnp.bfloat16), targets, weights
     )
-    summed_loss, slot_count = loss_tile[0, 0], loss_tile[1, 0]
     depth = rows // 2
     big = out_grad.reshape(depth, 2, groups, -1, inner)
     flat = jnp.concatenate(
@@ -754,112 +951,59 @@
     out_rows, small = reduce_all(
         big.transpose(1, 2, 0, 3, 4), small.reshape(2, groups, depth, piece, 128), groups, rows
     )
-    out_rows = out_rows.reshape(-1, inner).astype(jnp.float32)
-    small = small.reshape(-1, 128).astype(jnp.float32)
-    taps = tap_grads.shape[0]
-    tap_grads = jnp.concatenate(
-        [small[at * taps : (at + 1) * taps] for at in range(inner // 128)], axis=1
-    )
-    small = small[taps * (inner // 128) :]
-    count = wide_rows.shape[0]
-    wide_rows = jnp.concatenate(
-        [small[at * count : (at + 1) * count] for at in range(width // 128)], axis=1
-    )
-
-    weight_conv = weights[:, :, :own_conv].transpose(0, 2, 1).reshape(-1, inner)
-    weight_in = weights[:, :, own_conv : own_conv + own_in].transpose(0, 2, 1).reshape(-1, inner)
-    second_back = jax.vjp(norm_gelu, pre_inner, norm_rows[5, :inner], norm_rows[5, inner:])[1]
-    first_back = jax.vjp(norm_gelu, embedded, norm_rows[0], norm_rows[1])[1]
-    tap_view = tap_grads.reshape(CONV_TAPS, TABLE, inner)
-    second_grad = sum(
-        exact_dot(tap_view[tap], weight_conv[tap * inner : (tap + 1) * inner], (((1,), (1,)), ((), ())))
-        for tap in range(CONV_TAPS)
-    )
-    inner_pre, gain_two, bias_two = second_back(second_grad)
-    first_grad = exact_dot(inner_pre, weight_in, (((1,), (1,)), ((), ())))
-    table_grad, gain_one, bias_one = first_back(first_grad)
+    out_rows = out_rows.reshape(-1, inner)
+    in_rows, conv_rows, vec_sum, square_tile = table_step(
+        small.reshape(-1, 128), embedded, norm_rows, weights, pre_inner, first_low, placed, out_rows
+    )
     vec_sum = jnp.concatenate(
-        [
-            table_grad[:VOCAB] + wide_rows[:VOCAB],
-            wide_rows[TABLE : TABLE + VOCAB],
-            jnp.stack(
-                [
-                    gain_one,
-                    bias_one,
-                    wide_rows[2 * TABLE],
-                    wide_rows[2 * TABLE + 1],
-                    wide_rows[2 * TABLE + 2],
-                    jnp.concatenate([gain_two, bias_two]),
-                    jnp.concatenate(
-                        [jnp.sum(inner_pre, axis=0), jnp.sum(tap_view[CONV_TAPS // 2], axis=0)]
-                    ),
-                    wide_rows[2 * TABLE + 3],
-                ]
-            ),
-        ],
-        axis=0,
+        [vec_sum[:VOCAB], vec_sum[TABLE : TABLE + VOCAB], vec_sum[2 * TABLE :]], axis=0
     )
     own = width // (groups * rows)
     vec_own = lax.dynamic_slice_in_dim(vec_sum, (col_index * rows + row_index) * own, own, 1)
 
-    row_low = lax.dynamic_index_in_dim(first_low, row_index, 0, False)
-    in_rows = jnp.einsum(
-        "vr,vi->ri", row_low.astype(jnp.float32), inner_pre, precision=highest_precision
-    )
-    placed_own = lax.dynamic_index_in_dim(placed, row_index, 0, False)
-    conv_rows = jnp.einsum(
-        "vr,vi->ri", placed_own.astype(jnp.float32), tap_grads, precision=highest_precision
-    )
-
-    col_width = input_projection.shape[1]
-    col_start = col_index * col_width
-    owned = [
-        lax.dynamic_slice_in_dim(full_rows, col_start, col_width, 1)
-        for full_rows in (in_rows, conv_rows, out_rows)
-    ]
-    square_local = sum((jnp.sum(piece * piece) for piece in owned)) + jnp.sum(vec_own * vec_own)
-    square_total, summed_loss, slot_count = scalar_sums(
-        (square_local, summed_loss, slot_count), groups, rows
-    )
-    grad_norm = jnp.sqrt(square_total) / slot_count
+    tile = jnp.concatenate([square_tile[:1], loss_tile[:7]], axis=0)
+    sums = scalar_sums(tile, groups, rows)
+    slot_count = sums[2, 0]
+    grad_norm = jnp.sqrt(sums[0, 0]) / slot_count
     factor = jnp.minimum(1.0, clip_limit / grad_norm) / slot_count
-    step_value = optimizer_step[0].astype(jnp.float32)
-    first_correction = 1.0 - beta_one**step_value
-    second_correction = 1.0 - beta_two**step_value
-    identity = jnp.eye(bases.shape[1], dtype=jnp.float32)
-    rotated_grads = [
-        jnp.where(eigenbasis_flags[mat_index] == 1, bases[mat_index], identity)
-        for mat_index in range(3)
-    ]
-    master_in, copy_in, moment_in, square_in = eigenbasis_update(
-        in_rows * factor,
+    first_correction, second_correction = corrections(optimizer_step[0])
+    first_correction, second_correction = first_correction[0, 0], second_correction[0, 0]
+    master_in, copy_in, moment_in, square_in = matrix_update(
+        0,
+        False,
+        eigenbasis_flags,
+        optimizer_step,
+        sums,
+        in_rows,
+        bases,
         input_projection,
         input_first_moment,
         input_second_moment,
-        rotated_grads[0],
-        col_start,
-        first_correction,
-        second_correction,
-    )
-    updated_conv, conv_bfloat_copy, updated_conv_moment, updated_conv_square = eigenbasis_update(
-        conv_rows * factor,
-        dilated_conv,
+    )
+    updated_conv, conv_bfloat_copy, updated_conv_moment, updated_conv_square = matrix_update(
+        1,
+        True,
+        eigenbasis_flags,
+        optimizer_step,
+        sums,
+        conv_rows,
+        bases,
+        dilated_conv.T,
         conv_first_moment,
         conv_second_moment,
-        rotated_grads[1],
-        col_start,
-        first_correction,
-        second_correction,
-    )
-    master_out, copy_out, moment_out, square_out = eigenbasis_update(
-        out_rows * factor,
+    )
+    updated_conv, conv_bfloat_copy = updated_conv.T, conv_bfloat_copy.T
+    master_out, copy_out, moment_out, square_out = matrix_update(
+        2,
+        False,
+        eigenbasis_flags,
+        optimizer_step,
+        sums,
+        out_rows,
+        bases,
         output_projection,
         output_first_moment,
         output_second_moment,
-        rotated_grads[2],
-        col_start,
-        first_correction,
-        second_correction,
     )
     master_vec, copy_vec, moment_vec, square_vec = adam_vectors(
         vec_own * factor,
@@ -870,7 +1014,7 @@
         second_correction,
     )
     return (
-        summed_loss / slot_count,
+        sums[1, 0] / slot_count,
         grad_norm,
         master_in,
         copy_in,

time: 212 us -> 169 us (0.80)
  matrix products: 25.9 us -> 0 us
  local copies, waits for them, and re-layouts: 43.1 us -> 24.9 us
  Pallas kernels: 120 us -> 132 us
  other arithmetic: 8.36 us -> 2.92 us
  between operations: 13.3 us -> 8.27 us
    dot_general x20 -> x0, matrix products: 25.9 us -> none  [the longest x6 8.23 us: exact_dot(): lax.dot_general(high, right, contract, preferred_element_type=jnp.float32)]
    transpose x4 -> x0, local copies, waits for them, and re-layouts: 18.3 us -> none  [the longest x2 10.3 us: local(): weight_conv = weights[:, :, :own_conv].transpose(0, 2, 1).reshape(-1, inner)]
    pallas_call x0 -> x4, Pallas kernels: none -> 16.7 us  [the longest x3 13.7 us: matrix_update(): pl.pallas_call(partial(update_kernel, index, transposed), grid=(1,), out_...]
    reduce_sum x12 -> x0, other arithmetic: 4.15 us -> none  [the longest x3 2.22 us: local(): jnp.sum(piece * piece)]
    pallas_call x1, Pallas kernels: 18 us -> 14.6 us  [local_step(): pl.pallas_call(partial(local_step_kernel, min(slots, 128)), out_shape=(sh...]
    unnamed x109 -> x74, local copies, waits for them, and re-layouts: 16.1 us -> 19.3 us
where the time goes in v1:
time: 169 us; the launch traced here: 168 us
  Pallas kernels  132 us (78%)
  local copies, waits for them, and re-layouts  24.9 us (15%)
  between operations  8.27 us (5%)
  other arithmetic  2.92 us (2%)
    pallas_call x1, Pallas kernels, gather_all(): pl.pallas_call(partial(gather_kernel, dp_size, fsdp_size, cut), out_shape...  51.9 us
    pallas_call x1, Pallas kernels, reduce_all(): pl.pallas_call(partial(reduce_kernel, dp_size, fsdp_size), out_shape=(jax...  39.3 us
    unnamed x74, local copies, waits for them, and re-layouts  19.3 us
    pallas_call x1, Pallas kernels, local_step(): pl.pallas_call(partial(local_step_kernel, min(slots, 128)), out_shape=(sh...  14.6 us
    pallas_call x3, Pallas kernels, matrix_update(): pl.pallas_call(partial(update_kernel, index, transposed), grid=(1,), out_...  13.7 us
    pallas_call x1, Pallas kernels, scalar_sums(): pl.pallas_call(partial(scalar_kernel, dp_size, fsdp_size), out_shape=jax....  9.19 us

profile of v1, /device:TPU:0, one launch (start us, length us, event | category | flops | bytes accessed | tf_op | source)
XLA Modules:
  0.0 167.8 jit_solution(17787258867947671925)
XLA Ops:
  0.7 0.0 copy-start.20
  0.7 0.0 copy-start.21
  0.7 0.8 reshape.122
  1.5 0.8 reshape.123
  2.3 0.0 copy-start.4
  2.4 0.0 copy-start.8
  2.4 0.0 copy-start.7
  2.4 0.0 copy-done.20
  2.4 0.0 copy-done.21
  2.5 0.0 copy-start.17
  2.5 0.5 select_reduce_fusion.1
  3.0 0.1 iota_compare_fusion
  3.2 0.1 iota_compare_fusion.1
  3.3 0.1 iota_compare_fusion.2
  3.4 0.1 iota_compare_fusion.3
  3.5 0.1 iota_compare_fusion.4
  3.6 0.0 copy-start.22
  3.6 0.2 concatenate.59
  3.8 0.0 copy-done.4
  3.9 0.0 copy-done.8
  3.9 0.1 copy.61
  4.0 0.0 copy-done.7
  4.0 0.1 copy.62
  4.1 0.1 maximum_bitcast_fusion.shard_ref
  4.2 0.0 copy-done.17
  4.3 51.9 %gather_all.1 = (bf16[8,4,160,720]{3,2,1,0:T(8,128)(2,1)S(1)}, f32[4,8,40,68]{3,2,1,0:T(8,128)S(1)}) custom-call(bf16[160,720]{1,0:T(8,128)(2,1)S(1)} %maximum_bitcast_fusion.shard_ref, f32[40,68]{1,0:T(8,128)S(1)} %reduce-precision_bitcast_fusion.vec_ref), custom_call_target="tpu_custom_call" | custom-call | tf_op jit(solution)/shard_map/gather_all/pallas_call | solution.py:199
  56.2 0.0 copy-start.2
  56.2 3.0 %copy-done.2 = bf16[8,4,160,720]{3,2,1,0:T(8,128)(2,1)} copy-done((bf16[8,4,160,720]{3,2,1,0:T(8,128)(2,1)}, bf16[8,4,160,720]{3,2,1,0:T(8,128)(2,1)S(1)}, u32[]{:S(2)}) %copy-start.2) | copy-done | bytes 7372824
  59.3 0.2 copy.63
  59.5 0.0 copy-done.22
  59.5 0.1 slice_select_fusion.embed_ref
  59.7 0.1 copy.64.target_ref
  59.8 3.2 %copy-done.3 = bf16[8,4,160,720]{3,2,1,0:T(8,128)(2,1)S(1)} copy-done((bf16[8,4,160,720]{3,2,1,0:T(8,128)(2,1)S(1)}, bf16[8,4,160,720]{3,2,1,0:T(8,128)(2,1)}, u32[]{:S(2)}) %copy-start.3) | copy-done | bytes 7372824
  63.1 14.6 %local_step.1 = (bf16[8,160,640]{2,1,0:T(8,128)(2,1)S(1)}, f32[160,640]{1,0:T(8,128)S(1)}, f32[72,1280]{1,0:T(8,128)S(1)}, f32[8,128]{1,0:T(8,128)S(1)}, f32[32,...) custom-call(f32[32,1280]{1,0:T(8,128)S(1)} %slice_select_fusion.embed_ref, ...), custom_call_target="tpu_custom_call" | custom-call | tf_op jit(solution)/shard_map/local_step/pallas_call | solution.py:629
  77.9 0.1 copy.76
  78.1 39.3 %reduce_all.1 = (bf16[4,40,640]{2,1,0:T(8,128)(2,1)S(1)}, bf16[2,4,4,48,128]{4,3,2,1,0:T(8,128)(2,1)S(1)}) custom-call(bf16[2,4,4,40,640]{4,3,2,1,0:T(8,128)(2,1)S(1)} %bitcast.38, bf16[2,4,4,48,128]{4,3,2,1,0:T(8,128)(2,1)S(1)} %bitcast.44), custom_call_target="tpu_custom_call" | custom-call | tf_op jit(solution)/shard_map/reduce_all/pallas_call | solution.py:379
  117.4 0.0 copy-start.18
  117.4 0.0 copy-start.19
  117.4 3.0 %table_step.1 = (f32[160,640]{1,0:T(8,128)S(1)}, f32[400,640]{1,0:T(8,128)S(1)}, f32[72,1280]{1,0:T(8,128)S(1)}, f32[8,128]{1,0:T(8,128)S(1)}) custom-call(bf16[1536,128]{1,0:T(8,128)(2,1)S(1)} %bitcast.45, f32[32,1280]{1,0:T(8,128)S(1)} %slice_select_fusion.embed_ref, f32[8,1280]{1,0:T(8,128)S(1)} %slice.155.rows_ref, bf16[8,640,720]{2,1,0:T(8,128)(2,1)S(1)} %bitcast.37, ...), custom_call_target="tpu_custom_call" | custom-call | tf_op jit(solution)/shard_map/table_step/pallas_call | solution.py:754
  120.4 0.8 copy-done.13
  121.2 0.7 copy-done.15
  121.9 9.2 %scalar_sums.1.refs_2_ = f32[8,128]{1,0:T(8,128)S(1)} custom-call(f32[8,128]{1,0:T(8,128)S(1)} %pad_maximum_fusion.part_ref), custom_call_target="tpu_custom_call" | custom-call | tf_op jit(solution)/shard_map/scalar_sums/pallas_call | solution.py:451
  131.1 0.5 fusion.16
  133.7 0.0 slice-start
  133.8 1.8 %fusion.11 = (f32[30,1280]{1,0:T(8,128)}, f32[30,1280]{1,0:T(8,128)}) fusion(f32[72,1280]{1,0:T(8,128)} %copy-done.15), kind=kLoop, calls=%fused_computation.65 | loop fusion | bytes 614400 | tf_op jit(solution)/shard_map/slice | solution.py:959
  135.6 0.8 slice.152
  137.1 0.0 copy-done.18
  137.1 0.7 copy.66
  137.8 0.0 copy-done.19
  137.8 0.7 copy.68
  138.5 0.7 copy.70
  139.2 1.6 fusion.9
  140.8 1.5 copy.71
  142.2 0.7 copy.73
  142.9 0.7 copy.74
  143.6 1.4 copy.72
  145.0 0.0 copy-done.16
  145.0 0.0 copy-start
  145.0 2.4 %copy-done = f32[3,640,640]{2,1,0:T(8,128)S(1)} copy-done((f32[3,640,640]{2,1,0:T(8,128)S(1)}, f32[3,640,640]{2,1,0:T(8,128)}, u32[]{:S(2)}) %copy-start) | copy-done | bytes 4915224
  147.4 2.6 %update_2.1 = (f32[160,160]{1,0:T(8,128)}, bf16[160,160]{1,0:T(8,128)(2,1)}, f32[160,640]{1,0:T(8,128)}, f32[160,640]{1,0:T(8,128)}) custom-call(s32[3]{0:T(128)S(1)} %copy-done.16, s32[1]{0:T(128)S(6)} %copy.92.refs_1_, f32[8,128]{1,0:T(8,128)S(1)} %scalar_sums.1.refs_2_, bf16[160,640]{1,0:T(8,128)(2,1)S(1)} %bitcast.42, f32[3,640,640]{2,1,0:T(8,128)S(1)} %copy-done, ...), custom_call_target="tpu_custom_call" | custom-call | tf_op jit(solution)/shard_map/update_2/pallas_call | solution.py:863
  150.0 2.4 %copy-done.1 = f32[3,640,640]{2,1,0:T(8,128)S(1)} copy-done((f32[3,640,640]{2,1,0:T(8,128)S(1)}, f32[3,640,640]{2,1,0:T(8,128)}, u32[]{:S(2)}) %copy-start.1) | copy-done | bytes 4915224
  152.4 7.2 %update_1.1 = (f32[160,400]{1,0:T(8,128)}, bf16[160,400]{1,0:T(8,128)(2,1)}, f32[400,640]{1,0:T(8,128)}, f32[400,640]{1,0:T(8,128)}) custom-call(s32[3]{0:T(128)S(1)} %copy-done.16, s32[1]{0:T(128)S(6)} %copy.92.refs_1_, f32[8,128]{1,0:T(8,128)S(1)} %scalar_sums.1.refs_2_, f32[400,640]{1,0:T(8,128)S(1)} %get-tuple-element.62.refs_3_, ...), custom_call_target="tpu_custom_call" | custom-call | tf_op jit(solution)/shard_map/update_1/pallas_call | solution.py:863
  159.7 0.0 slice-done.1
  159.7 3.9 %update_0.1 = (f32[160,160]{1,0:T(8,128)}, bf16[160,160]{1,0:T(8,128)(2,1)}, f32[160,640]{1,0:T(8,128)}, f32[160,640]{1,0:T(8,128)}) custom-call(s32[3]{0:T(128)S(1)} %copy-done.16, s32[1]{0:T(128)S(6)} %copy.92.refs_1_, f32[8,128]{1,0:T(8,128)S(1)} %scalar_sums.1.refs_2_, f32[160,640]{1,0:T(8,128)S(1)} %copy-done.14, f32[3,640,640]{2,1,0:T(8,128)S(1)} %bitcast.35, ...), custom_call_target="tpu_custom_call" | custom-call | tf_op jit(solution)/shard_map/update_0/pallas_call | solution.py:863
  (55 shorter events, 0.4 us)
Async XLA Ops:
  0.7 1.8 %copy-start.20 = (s32[2,128]{1,0:T(2,128)S(1)}, s32[2,128]{1,0:T(2,128)}, u32[]{:S(2)}) copy-start(s32[2,128]{1,0:T(2,128)} %param.21) | copy-start | bytes 3076
  0.7 1.8 %copy-start.21 = (s32[2,128]{1,0:T(2,128)S(1)}, s32[2,128]{1,0:T(2,128)}, u32[]{:S(2)}) copy-start(s32[2,128]{1,0:T(2,128)} %param.22) | copy-start | bytes 3076
  2.3 1.5 copy-start.4
  2.4 1.5 copy-start.8
  2.4 1.6 copy-start.7
  2.5 1.8 %copy-start.17 = (f32[68,40]{0,1:T(8,128)S(1)}, f32[68,40]{0,1:T(8,128)}, u32[]{:S(2)}) copy-start(f32[68,40]{0,1:T(8,128)} %param.26) | copy-start | bytes 32644
  3.6 55.9 %copy-start.22 = (pred[32]{0:T(512)(128)(4,1)S(1)}, pred[32]{0:T(512)(128)(4,1)}, u32[]{:S(2)}) copy-start(pred[32]{0:T(512)(128)(4,1)} %constant.23.clone.1) | copy-start | bytes 100
  56.2 3.1 %copy-start.2 = (bf16[8,4,160,720]{3,2,1,0:T(8,128)(2,1)}, bf16[8,4,160,720]{3,2,1,0:T(8,128)(2,1)S(1)}, u32[]{:S(2)}) copy-start(bf16[8,4,160,720]{3,2,1,0:T(8,128)(2,1)S(1)} %get-tuple-element.46) | copy-start | bytes 22118404
  59.8 3.2 %copy-start.3 = (bf16[8,4,160,720]{3,2,1,0:T(8,128)(2,1)S(1)}, bf16[8,4,160,720]{3,2,1,0:T(8,128)(2,1)}, u32[]{:S(2)}) copy-start(bf16[8,4,160,720]{3,2,1,0:T(8,128)(2,1)} %copy-done.2) | copy-start | bytes 22118404
  117.4 19.7 %copy-start.18 = (f32[68,40]{0,1:T(8,128)S(1)}, f32[68,40]{0,1:T(8,128)}, u32[]{:S(2)}) copy-start(f32[68,40]{0,1:T(8,128)} %param.33) | copy-start | bytes 32644
  117.4 20.4 %copy-start.19 = (f32[68,40]{0,1:T(8,128)S(1)}, f32[68,40]{0,1:T(8,128)}, u32[]{:S(2)}) copy-start(f32[68,40]{0,1:T(8,128)} %param.34) | copy-start | bytes 32644
  120.4 0.8 copy-start.13
  121.2 0.7 copy-start.15
  121.9 23.1 %copy-start.9 = (f32[160,640]{1,0:T(8,128)S(1)}, f32[160,640]{1,0:T(8,128)}, u32[]{:S(2)}) copy-start(f32[160,640]{1,0:T(8,128)} %refs_6_.5) | copy-start | bytes 1228804
  121.9 23.1 %copy-start.10 = (f32[160,640]{1,0:T(8,128)S(1)}, f32[160,640]{1,0:T(8,128)}, u32[]{:S(2)}) copy-start(f32[160,640]{1,0:T(8,128)} %refs_7_.5) | copy-start | bytes 1228804
  121.9 23.1 %copy-start.16 = (s32[3]{0:T(128)S(1)}, s32[3]{0:T(128)}, u32[]{:S(2)}) copy-start(s32[3]{0:T(128)} %refs_0_.5) | copy-start | bytes 40
  133.7 25.9 %slice-start = ((s8[4915200]{0:T(1024)(128)(4,1)}), s8[720896]{0:T(1024)(128)(4,1)S(1)}, s32[]{:S(2)}) async-start(s8[4915200]{0:T(1024)(128)(4,1)} %bitcast.34), calls=%async_computation | async-start | bytes 1441792
  145.0 2.4 %copy-start = (f32[3,640,640]{2,1,0:T(8,128)S(1)}, f32[3,640,640]{2,1,0:T(8,128)}, u32[]{:S(2)}) copy-start(f32[3,640,640]{2,1,0:T(8,128)} %refs_4_.5) | copy-start | bytes 14745604
  147.4 2.6 %copy-start.5 = (f32[400,640]{1,0:T(8,128)S(1)}, f32[400,640]{1,0:T(8,128)}, u32[]{:S(2)}) copy-start(f32[400,640]{1,0:T(8,128)} %refs_6_.4) | copy-start | bytes 3072004
  147.4 2.6 %copy-start.6 = (f32[400,640]{1,0:T(8,128)S(1)}, f32[400,640]{1,0:T(8,128)}, u32[]{:S(2)}) copy-start(f32[400,640]{1,0:T(8,128)} %refs_7_.4) | copy-start | bytes 3072004
  150.0 2.4 %copy-start.1 = (f32[3,640,640]{2,1,0:T(8,128)S(1)}, f32[3,640,640]{2,1,0:T(8,128)}, u32[]{:S(2)}) copy-start(f32[3,640,640]{2,1,0:T(8,128)} %refs_4_.5) | copy-start | bytes 14745604
  152.4 7.2 %slice-start.1 = ((s8[4915200]{0:T(1024)(128)(4,1)}), s8[4194304]{0:T(1024)(128)(4,1)S(1)}, s32[]{:S(2)}) async-start(s8[4915200]{0:T(1024)(128)(4,1)} %bitcast.34), calls=%async_computation.1 | async-start | bytes 8388608
  152.4 7.2 %copy-start.11 = (f32[160,640]{1,0:T(8,128)S(1)}, f32[160,640]{1,0:T(8,128)}, u32[]{:S(2)}) copy-start(f32[160,640]{1,0:T(8,128)} %refs_6_.3) | copy-start | bytes 1228804
  152.4 7.3 %copy-start.12 = (f32[160,640]{1,0:T(8,128)S(1)}, f32[160,640]{1,0:T(8,128)}, u32[]{:S(2)}) copy-start(f32[160,640]{1,0:T(8,128)} %refs_7_.3) | copy-start | bytes 1228804
  152.4 7.3 %copy-start.14 = (f32[160,640]{1,0:T(8,128)S(1)}, f32[160,640]{1,0:T(8,128)}, u32[]{:S(2)}) copy-start(f32[160,640]{1,0:T(8,128)} %copy-done.13) | copy-start | bytes 1228804
